TPU v7x, 128 devices: a whole 4x4x4 slice. The times are simulated.
128 devices in a mesh: dom: 32 (over x, y, core), grp: 4 (over z).
Axes of the slice: x: 4, y: 4, z: 4, core: 2. Of those that a mesh axis runs over, the one named last changes fastest.
Arguments:
- features: bfloat16 [262144, 256], P(('dom', 'grp')), may hold values from -6 to 6
- edge_src: int32 [2097152], P(('dom', 'grp')), may hold values from 0 to 3071, as said below
- edge_dst: int32 [2097152], P(('dom', 'grp')), may hold values from 0 to 2047, as said below
- edge_count: int32 [128], P(('dom', 'grp')), may hold values from 4096 to 16384, as said below
- halo_index: int32 [128, 128, 8], P(('dom', 'grp')), may hold values from 0 to 2047
- request_rows: int32 [128, 128, 16], P(('dom', 'grp')), may hold values from 0 to 2047, as said below
- pair_ends: int32 [262144, 2], P(('dom', 'grp')), may hold values from 0 to 2047
- labels: int32 [262144], P(('dom', 'grp')), may hold values 0 or 1
- pair_weight: float32 [262144], P(('dom', 'grp')), may hold values from 0.25 to 4
- w_self: bfloat16 [256, 256], replicated, may hold values from -0.375 to 0.375
- w_neigh: bfloat16 [256, 256], replicated, may hold values from -0.375 to 0.375
- w_hidden: bfloat16 [512, 256], replicated, may hold values from -0.25 to 0.25
- b_hidden: float32 [256], replicated, may hold values from -3 to 3
- w_out: float32 [256], replicated, may hold values from -0.375 to 0.375
Outputs:
- logits: float32 [262144], P(('dom', 'grp'))
- grad_features: float32 [262144, 256], P(('dom', 'grp'))
- grad_w_self: float32 [256, 256], replicated
- grad_w_neigh: float32 [256, 256], replicated
- grad_w_hidden: float32 [512, 256], replicated
- grad_b_hidden: float32 [256], replicated
- grad_w_out: float32 [256], replicated
Inputs may be any that keep to these rules, and one draw needn't show every extreme that they name: `edge_src`: a row of the partition's own table. `edge_dst`: a local node of the partition; slots at or past edge_count are not live and hold arbitrary values. `edge_count`: some partition has exactly 16384 live slots. `halo_index`: local rows of the sending partition; 8 to every partition, itself included. `request_rows`: local rows of the owning partition, distinct and increasing within each list of 16. `pair_ends`: rows of the shard's own received rows.
All inputs are finite; a program needn't handle non-finite values. No bound on the sum of `labels` on one device may be relied on, other than what follows from the above.
Results may differ from a plain program's by a relative error of at most 0.02.
The roundings to bfloat16 on the way count: a program that leaves them out, or rounds other values in their place, can miss the bound.
Values may be sent and summed in bfloat16 or wider, within the bound.
No kernel may reach another device: no remote copies, remote signals or barrier semaphores. Data moves between devices by JAX's collectives and lax.ppermute only.
A program may use at most 192 MiB of HBM per device.

v0:
```python
import jax
import jax.numpy as jnp
from jax import lax
from jax.sharding import PartitionSpec as P


def in_one(arrays, axis):
    vector, at, outs = (jnp.concatenate([a.reshape(-1) for a in arrays]), 0, [])
    total = lax.psum(vector, axis)
    for a in arrays:
        outs.append(total[at : at + a.size].reshape(a.shape))
        at += a.size
    return tuple(outs)


def contract_rows(left, right):
    return lax.dot_general(
        left, right, (((0,), (0,)), ((), ())), preferred_element_type=jnp.float32
    )


def per_device(
    features,
    edge_src,
    edge_dst,
    edge_count,
    halo_index,
    request_rows,
    pair_ends,
    labels,
    pair_weight,
    w_self,
    w_neigh,
    w_hidden,
    b_hidden,
    w_out,
):
    node_rows, feat_width = features.shape
    dom_count = lax.axis_size("dom")
    grp_count = lax.axis_size("grp")
    peer_count = dom_count * grp_count
    halo_len = halo_index.shape[2]
    outgoing = features[halo_index[0]]
    arrived = lax.all_to_all(outgoing, ("dom", "grp"), split_axis=0, concat_axis=0, tiled=True)
    row_table = jnp.concatenate(
        [features, arrived.reshape(peer_count * halo_len, feat_width)], axis=0
    )
    table_rows = row_table.shape[0]
    slot_total = edge_src.shape[0]
    alive_slot = jnp.arange(slot_total, dtype=jnp.int32) < edge_count[0]
    dst_index = jnp.where(alive_slot, edge_dst, node_rows)
    adjacency = (
        jnp.zeros((node_rows + 1, table_rows), jnp.float32)
        .at[dst_index, edge_src]
        .add(1.0)[:node_rows]
    )
    degree = jnp.sum(adjacency, axis=1)
    floor_deg = jnp.maximum(degree, 1.0)[:, None]
    agg_sums = jnp.dot(adjacency, row_table.astype(jnp.float32))
    aggregate = (agg_sums / floor_deg).astype(jnp.bfloat16)
    embedding = (
        jnp.dot(features, w_self, preferred_element_type=jnp.float32)
        + jnp.dot(aggregate, w_neigh, preferred_element_type=jnp.float32)
    ).astype(jnp.bfloat16)
    wanted = lax.all_to_all(
        request_rows[0], ("dom", "grp"), split_axis=0, concat_axis=0, tiled=True
    )
    req_len = wanted.shape[1]
    served = embedding[wanted]
    received = lax.all_to_all(served, ("dom", "grp"), split_axis=0, concat_axis=0, tiled=True)
    recv_rows = peer_count * req_len
    received = received.reshape(recv_rows, feat_width)
    slot_ids = jnp.arange(recv_rows, dtype=jnp.int32)[None, :]
    select_left = (pair_ends[:, 0][:, None] == slot_ids).astype(jnp.float32)
    select_right = (pair_ends[:, 1][:, None] == slot_ids).astype(jnp.float32)
    left_rows = jnp.dot(
        select_left.astype(jnp.bfloat16), received, preferred_element_type=jnp.float32
    ).astype(jnp.bfloat16)
    right_rows = jnp.dot(
        select_right.astype(jnp.bfloat16), received, preferred_element_type=jnp.float32
    ).astype(jnp.bfloat16)
    pair_input = jnp.concatenate([left_rows, right_rows], axis=1)
    pre_act = jnp.dot(pair_input, w_hidden, preferred_element_type=jnp.float32) + b_hidden
    hidden = jnp.maximum(pre_act, 0.0)
    logits = jnp.dot(hidden, w_out)
    slope_term = pair_weight * (jax.nn.sigmoid(logits) - labels.astype(jnp.float32))
    grad_out = jnp.dot(slope_term, hidden)
    delta_act = jnp.where(pre_act > 0, slope_term[:, None] * w_out[None, :], 0.0)
    grad_bias = jnp.sum(delta_act, axis=0)
    delta_b = delta_act.astype(jnp.bfloat16)
    grad_hidden = jnp.dot(pair_input.T, delta_b, preferred_element_type=jnp.float32)
    pair_grad = jnp.dot(delta_b, w_hidden.T, preferred_element_type=jnp.float32)
    received_grad = contract_rows(select_left, pair_grad[:, :feat_width]) + contract_rows(
        select_right, pair_grad[:, feat_width:]
    )
    received_grad_b = received_grad.astype(jnp.bfloat16)
    back_rows = lax.all_to_all(
        received_grad_b.reshape(peer_count, req_len, feat_width),
        ("dom", "grp"),
        split_axis=0,
        concat_axis=0,
        tiled=True,
    )
    embedding_grad = (
        jnp.zeros((node_rows, feat_width), jnp.float32)
        .at[wanted.reshape(recv_rows)]
        .add(back_rows.reshape(recv_rows, feat_width).astype(jnp.float32))
    )
    grad_b = embedding_grad.astype(jnp.bfloat16)
    grad_self = jnp.dot(features.T, grad_b, preferred_element_type=jnp.float32)
    grad_neigh = jnp.dot(aggregate.T, grad_b, preferred_element_type=jnp.float32)
    direct = jnp.dot(grad_b, w_self.T, preferred_element_type=jnp.float32)
    agg_grad = jnp.dot(grad_b, w_neigh.T, preferred_element_type=jnp.float32) / floor_deg
    table_grad = contract_rows(adjacency, agg_grad)
    returned = table_grad[node_rows:].reshape(peer_count, halo_len, feat_width)
    halo_back = lax.all_to_all(
        returned.astype(jnp.bfloat16), ("dom", "grp"), split_axis=0, concat_axis=0, tiled=True
    ).astype(returned.dtype)
    grad_features = (
        (direct + table_grad[:node_rows])
        .at[halo_index[0].reshape(peer_count * halo_len)]
        .add(halo_back.reshape(peer_count * halo_len, feat_width))
    )
    summed = in_one((grad_self, grad_neigh, grad_hidden, grad_bias, grad_out), ("dom", "grp"))
    return (logits, grad_features, summed[0], summed[1], summed[2], summed[3], summed[4])


def solution(mesh):
    in_specs = (
        P(("dom", "grp"), None),
        P(("dom", "grp")),
        P(("dom", "grp")),
        P(("dom", "grp")),
        P(("dom", "grp"), None, None),
        P(("dom", "grp"), None, None),
        P(("dom", "grp"), None),
        P(("dom", "grp")),
        P(("dom", "grp")),
        P(),
        P(),
        P(),
        P(),
        P(),
    )
    out_specs = (P(("dom", "grp")), P(("dom", "grp"), None), P(), P(), P(), P(), P())
    return jax.shard_map(
        per_device, mesh=mesh, in_specs=in_specs, out_specs=out_specs, check_vma=False
    )
```

profile of v0, /device:TPU:1, one launch (start us, length us, event | category | flops | bytes accessed | tf_op | source)
XLA Modules:
  0.0 484.7 jit_solution(14658335759810923802)
XLA Ops:
  7.2 1.5 copy.31
  8.7 11.5 %all-to-all-start.1 = ((s32[128,1,16]{2,1,0:T(1,128)}), s32[128,1,16]{2,1,0:T(1,128)S(1)}, u32[]{:S(2)}, u32[]{:S(2)}) async-start(s32[128,1,16]{2,1,0:T(1,128)} %bitcast.7), calls=%async_computation.1 | async-start | bytes 131072 | tf_op jit(solution)/shard_map/all_to_all | solution.py:65
  20.8 0.9 compare_select_fusion.1
  21.6 0.9 compare_select_fusion.2
  22.5 0.9 multiply_reduce_fusion
  23.4 1.0 and_reduce_fusion
  24.4 0.7 compare_select_fusion.5
  25.3 3.0 fusion.59
  28.3 95.7 %scatter_custom_fusion.2 = f32[6294528]{0:T(1024)} fusion(s32[16384]{0:T(1024)S(1)} %broadcast_select_fusion, f32[16384]{0:T(1024)S(1)} %broadcast.84, f32[]{:T(128)} %constant.6.clone.1), kind=kCustom, calls=%fused_computation.11 | custom fusion | flops 16384 | bytes 25178116
  124.0 16.7 %slice.87 = f32[6291456]{0:T(1024)} slice(f32[6294528]{0:T(1024)} %scatter_custom_fusion.2), slice={[0:6291456]} | slice | bytes 50331648 | tf_op jit(solution)/shard_map/slice | solution.py:53
  140.8 27.1 %reshape.208 = f32[2048,3072]{1,0:T(8,128)} reshape(f32[6291456]{0:T(1024)} %slice.87) | data formatting | bytes 50331648 | tf_op jit(solution)/shard_map/slice | solution.py:53
  167.9 9.2 %reduce_sum.18 = f32[2048]{0:T(1024)S(1)} reduce(f32[2048,3072]{1,0:T(8,128)} %reshape.208, f32[]{:T(128)} %constant.6.clone.1), dimensions={1}, to_apply=%region_1.2 | reduce | flops 6289408 | bytes 25174020 | tf_op jit(solution)/shard_map/reduce_sum | solution.py:57
  177.1 5.0 %gather_fusion = bf16[1024,256]{1,0:T(8,128)(2,1)} fusion(bf16[2048,256]{1,0:T(8,128)(2,1)S(1)} %copy-done.1, s32[1024]{0:T(1024)S(1)} %broadcast_clamp_fusion.1), kind=kCustom, calls=%fused_computation | custom fusion | bytes 1052672 | tf_op jit(solution)/shard_map/gather | solution.py:43
  182.1 10.4 %all-to-all-start = ((bf16[128,8,256]{2,1,0:T(8,128)(2,1)}), bf16[128,8,256]{2,1,0:T(8,128)(2,1)S(1)}, u32[]{:S(2)}, u32[]{:S(2)}) async-start(bf16[128,8,256]{2,1,0:T(8,128)(2,1)} %bitcast.5), calls=%async_computation | async-start | bytes 1048576 | tf_op jit(solution)/shard_map/all_to_all | solution.py:44
  192.6 13.7 %all-to-all-done = bf16[128,8,256]{2,1,0:T(8,128)(2,1)S(1)} async-done(((bf16[128,8,256]{2,1,0:T(8,128)(2,1)}), bf16[128,8,256]{2,1,0:T(8,128)(2,1)S(1)}, u32[]{:S(2)}, u32[]{:S(2)}) %all-to-all-start) | async-done | bytes 524320 | tf_op jit(solution)/shard_map/all_to_all | solution.py:44
  206.3 11.9 %fusion.15 = bf16[2048,256]{1,0:T(8,128)(2,1)S(1)} fusion(f32[2048,3072]{1,0:T(8,128)} %reshape.208, bf16[1024,256]{1,0:T(8,128)(2,1)S(1)} %bitcast.67, bf16[2048,256]{1,0:T(8,128)(2,1)S(1)} %copy-done.1, f32[2048]{0:T(1024)S(1)} %broadcast_maximum_fusion), kind=kOutput, calls=%fused_computation.29 | convolution fusion | flops 3225419776 | bytes 27795456 | tf_op jit(solution)/shard_map/dot_general | solution.py:59
  218.6 9.1 %gather_fusion.1 = bf16[2048,256]{1,0:T(8,128)(2,1)} fusion(bf16[2048,256]{1,0:T(8,128)(2,1)S(1)} %fusion.12, s32[2048]{0:T(1024)S(1)} %broadcast_clamp_fusion), kind=kCustom, calls=%fused_computation.1 | custom fusion | bytes 2105344 | tf_op jit(solution)/shard_map/gather | solution.py:69
  227.7 4.1 all-to-all-start.2
  231.8 19.5 %all-to-all-done.2 = bf16[128,16,256]{2,1,0:T(8,128)(2,1)S(1)} async-done(((bf16[128,16,256]{2,1,0:T(8,128)(2,1)}), bf16[128,16,256]{2,1,0:T(8,128)(2,1)S(1)}, u32[]{:S(2)}, u32[]{:S(2)}) %all-to-all-start.2) | async-done | bytes 1048608 | tf_op jit(solution)/shard_map/all_to_all | solution.py:70
  251.3 2.9 fusion.13
  254.2 3.1 fusion.14
  257.4 0.7 convolution_add_fusion
  259.1 1.1 fusion.21
  260.2 0.8 fusion.33
  261.0 4.9 %fusion = f32[2048,256]{1,0:T(8,128)S(1)} fusion(s32[2048]{0:T(1024)S(1)} %bitcast.87, bf16[2048,512]{1,0:T(8,128)(2,1)S(1)} %fusion.33), kind=kOutput, calls=%fused_computation.7 | convolution fusion | flops 2151677952 | bytes 3153920 | tf_op jit(solution)/shard_map/dot_general | solution.py:17
  265.9 6.2 %fusion.11 = bf16[2048,256]{1,0:T(8,128)(2,1)} fusion(f32[2048,256]{1,0:T(8,128)S(1)} %fusion, s32[2048]{0:T(1024)S(1)} %bitcast.85, bf16[2048,512]{1,0:T(8,128)(2,1)S(1)} %fusion.33), kind=kOutput, calls=%fused_computation.24 | convolution fusion | flops 2152726528 | bytes 4202496 | tf_op jit(solution)/shard_map/dot_general | solution.py:17
  272.2 3.9 all-to-all-start.3
  276.1 0.8 copy.32
  276.9 0.7 reshape_squeeze.3
  278.1 0.8 reduce.7
  279.1 2.7 fusion.31
  281.8 1.1 copy.36
  283.1 12.5 %all-to-all-done.3 = bf16[128,16,256]{2,1,0:T(8,128)(2,1)S(1)} async-done(((bf16[128,16,256]{2,1,0:T(8,128)(2,1)}), bf16[128,16,256]{2,1,0:T(8,128)(2,1)S(1)}, u32[]{:S(2)}, u32[]{:S(2)}) %all-to-all-start.3) | async-done | bytes 1048608 | tf_op jit(solution)/shard_map/all_to_all | solution.py:97
  295.6 13.0 %scatter_custom_fusion = f32[2048,256]{1,0:T(8,128)} fusion(s32[2048]{0:T(1024)S(1)} %bitcast.83, bf16[2048,256]{1,0:T(8,128)(2,1)S(1)} %bitcast.66, f32[]{:T(128)} %constant.6.clone.1), kind=kCustom, calls=%fused_computation.34 | custom fusion | flops 1048576 | bytes 3145732 | tf_op jit(solution)/shard_map/scatter-add | solution.py:107
  308.6 1.7 convert_element_type.61
  310.4 1.2 convolution_bitcast_fusion
  312.0 12.3 %fusion.16 = f32[3072,256]{1,0:T(8,128)} fusion(f32[2048,3072]{1,0:T(8,128)} %reshape.208, bf16[2048,256]{1,0:T(8,128)(2,1)S(1)} %convert_element_type.61, bf16[256,256]{1,0:T(8,128)(2,1)S(1)} %copy-done.10, f32[2048]{0:T(1024)S(1)} %broadcast_maximum_fusion), kind=kOutput, calls=%fused_computation.30 | convolution fusion | flops 3490185216 | bytes 29499392 | tf_op jit(solution)/shard_map/dot_general | solution.py:17
  325.5 1.0 copy-done.6
  326.5 2.1 fusion.47
  328.6 4.3 all-to-all-start.4
  332.9 3.4 convolution_add_fusion.1
  336.3 10.8 %all-to-all-done.4 = bf16[128,8,256]{2,1,0:T(8,128)(2,1)S(1)} async-done(((bf16[128,8,256]{2,1,0:T(8,128)(2,1)}), bf16[128,8,256]{2,1,0:T(8,128)(2,1)S(1)}, u32[]{:S(2)}, u32[]{:S(2)}) %all-to-all-start.4) | async-done | bytes 524320 | tf_op jit(solution)/shard_map/all_to_all | solution.py:116
  347.1 9.0 %scatter_custom_fusion.1 = f32[2048,256]{1,0:T(8,128)} fusion(f32[2048,256]{1,0:T(8,128)} %convolution_add_fusion.1, s32[1024]{0:T(1024)S(1)} %bitcast.90, bf16[128,8,256]{2,1,0:T(8,128)(2,1)S(1)} %all-to-all-done.4), kind=kCustom, calls=%fused_computation.52 | custom fusion | flops 524288 | bytes 2621440 | tf_op jit(solution)/shard_map/scatter-add | solution.py:122
  356.1 117.2 %all-reduce.2.cloned.1.call-done = f32[262656]{0:T(1024)} async-done(((f32[262656]{0:T(1024)}), f32[262656]{0:T(1024)}) %all-reduce.2.cloned.1.call-update) | async-done | bytes 1050640 | tf_op jit(solution)/shard_map/psum | solution.py:9
  473.3 1.2 slice.94
  474.4 0.9 slice.79
  475.4 0.8 slice.75
  476.2 0.8 slice.77
  (77 shorter events, 4.9 us)
Async XLA Ops:
  7.2 250.2 %copy-start = (bf16[512,256]{1,0:T(8,128)(2,1)S(1)}, bf16[512,256]{1,0:T(8,128)(2,1)}, u32[]{:S(2)}) copy-start(bf16[512,256]{1,0:T(8,128)(2,1)} %param.25) | copy-start | bytes 786436
  8.7 173.4 %all-to-all-start.1 = ((s32[128,1,16]{2,1,0:T(1,128)}), s32[128,1,16]{2,1,0:T(1,128)S(1)}, u32[]{:S(2)}, u32[]{:S(2)}) async-start(s32[128,1,16]{2,1,0:T(1,128)} %bitcast.7), calls=%async_computation.1 | async-start | bytes 131072 | tf_op jit(solution)/shard_map/all_to_all | solution.py:65
  167.9 9.2 %copy-start.1 = (bf16[2048,256]{1,0:T(8,128)(2,1)S(1)}, bf16[2048,256]{1,0:T(8,128)(2,1)}, u32[]{:S(2)}) copy-start(bf16[2048,256]{1,0:T(8,128)(2,1)} %param.14) | copy-start | bytes 3145732
  182.1 24.2 %all-to-all-start = ((bf16[128,8,256]{2,1,0:T(8,128)(2,1)}), bf16[128,8,256]{2,1,0:T(8,128)(2,1)S(1)}, u32[]{:S(2)}, u32[]{:S(2)}) async-start(bf16[128,8,256]{2,1,0:T(8,128)(2,1)} %bitcast.5), calls=%async_computation | async-start | bytes 1048576 | tf_op jit(solution)/shard_map/all_to_all | solution.py:44
  206.3 11.9 %copy-start.4 = (f32[2048,256]{1,0:T(8,128)S(1)}, f32[2048,256]{1,0:T(8,128)}, u32[]{:S(2)}) copy-start(f32[2048,256]{1,0:T(8,128)} %fusion.59) | copy-start | bytes 6291460
  206.3 11.9 %copy-start.9 = (bf16[256,256]{1,0:T(8,128)(2,1)S(1)}, bf16[256,256]{1,0:T(8,128)(2,1)}, u32[]{:S(2)}) copy-start(bf16[256,256]{1,0:T(8,128)(2,1)} %param.24) | copy-start | bytes 393220
  227.7 4.1 copy-start.15
  227.7 23.7 %all-to-all-start.2 = ((bf16[128,16,256]{2,1,0:T(8,128)(2,1)}), bf16[128,16,256]{2,1,0:T(8,128)(2,1)S(1)}, u32[]{:S(2)}, u32[]{:S(2)}) async-start(bf16[128,16,256]{2,1,0:T(8,128)(2,1)} %bitcast.65), calls=%async_computation.2 | async-start | bytes 2097152 | tf_op jit(solution)/shard_map/all_to_all | solution.py:70
  254.2 3.1 copy-start.21
  254.2 3.1 copy-start.20
  257.4 1.0 copy-start.22
  257.4 1.0 copy-start.18
  258.4 1.9 copy-start.2
  258.4 0.7 copy-start.16
  258.4 0.8 copy-start.17
  258.7 2.2 copy-start.13
  260.2 5.7 %copy-start.11 = (pred[2048,256]{1,0:T(32,128)(4,1)}, pred[2048,256]{1,0:T(32,128)(4,1)S(1)}, u32[]{:S(2)}) copy-start(pred[2048,256]{1,0:T(32,128)(4,1)S(1)} %get-tuple-element.8) | copy-start | bytes 1572868
  272.2 23.4 %all-to-all-start.3 = ((bf16[128,16,256]{2,1,0:T(8,128)(2,1)}), bf16[128,16,256]{2,1,0:T(8,128)(2,1)S(1)}, u32[]{:S(2)}, u32[]{:S(2)}) async-start(bf16[128,16,256]{2,1,0:T(8,128)(2,1)} %bitcast.69), calls=%async_computation.3 | async-start | bytes 2097152 | tf_op jit(solution)/shard_map/all_to_all | solution.py:97
  276.1 197.2 %all-reduce.2.cloned.1.call-start = ((), (), s32[]{:S(2)}) async-start(), calls=%async_computation.5 | async-start | bytes 2105344 | tf_op jit(solution)/shard_map/psum | solution.py:9
  279.1 3.8 copy-start.3
  310.3 1.7 copy-start.10
  312.0 12.3 %copy-start.8 = (f32[32,2,8,128]{3,2,1,0:T(8,128)S(1)}, f32[32,2,8,128]{3,2,1,0:T(8,128)}, u32[]{:S(2)}) copy-start(f32[32,2,8,128]{3,2,1,0:T(8,128)} %convolution_bitcast_fusion) | copy-start | bytes 786436
  324.3 1.0 copy-start.5
  324.3 1.1 copy-start.19
  325.4 7.5 %copy-start.14 = (s32[1024,1]{0,1:T(1,128)S(1)}, s32[1024,1]{0,1:T(1,128)}, u32[]{:S(2)}) copy-start(s32[1024,1]{0,1:T(1,128)} %reshape_squeeze.3) | copy-start | bytes 12292
  325.4 7.5 %copy-start.12 = (bf16[256,256]{1,0:T(8,128)(2,1)S(1)}, bf16[256,256]{1,0:T(8,128)(2,1)}, u32[]{:S(2)}) copy-start(bf16[256,256]{1,0:T(8,128)(2,1)} %param.23) | copy-start | bytes 393220
  325.5 1.0 copy-start.6
  328.6 18.5 %all-to-all-start.4 = ((bf16[128,8,256]{2,1,0:T(8,128)(2,1)}), bf16[128,8,256]{2,1,0:T(8,128)(2,1)S(1)}, u32[]{:S(2)}, u32[]{:S(2)}) async-start(bf16[128,8,256]{2,1,0:T(8,128)(2,1)} %fusion.47), calls=%async_computation.4 | async-start | bytes 1048576 | tf_op jit(solution)/shard_map/all_to_all | solution.py:116
  473.3 2.1 copy-start.7
Sparse Core Ops, SparseCore 0:
  326.6 146.6 all-reduce.1
where the time goes:
time: 492 us; the launch traced here: 485 us
  waiting for transfers between devices  174 us (35%)
  other arithmetic  135 us (27%)
  local copies, waits for them, and re-layouts  71.9 us (15%)
  matrix products  54.6 us (11%)
  starting transfers between devices  34.2 us (7%)
  between operations  15.4 us (3%)
    psum x1, waiting for transfers between devices, in_one(): total = lax.psum(vector, axis)  117 us
    unnamed x4, other arithmetic  97.6 us
    slice x2, local copies, waits for them, and re-layouts, per_device(): jnp.zeros((node_rows + 1, table_rows), jnp.float32).at[dst_index, edge_src]  43.9 us
    dot_general x3, matrix products, contract_rows(): lax.dot_general(left, right, (((0,), (0,)), ((), ())), preferred_element_...  23.5 us
    all_to_all x1, waiting for transfers between devices, per_device(): lax.all_to_all(served, ('dom', 'grp'), split_axis=0, concat_axis=0, tiled...  19.5 us
    all_to_all x1, waiting for transfers between devices, per_device(): lax.all_to_all(outgoing, ('dom', 'grp'), split_axis=0, concat_axis=0, til...  13.7 us
    scatter-add x1, other arithmetic, per_device(): embedding_grad = jnp.zeros((node_rows, feat_width), jnp.float32).at[wante...  13 us
    all_to_all x1, waiting for transfers between devices, per_device(): lax.all_to_all(received_grad_b.reshape(peer_count, req_len, feat_width),...  12.5 us
  transfers between devices with their start and end apart: 6, of which 5 were waited for; matrix products, arithmetic and copies ran while one was open for 38% of the time, Pallas kernels for 0%

commit v1 on v0

--- a/solution.py
+++ b/solution.py
@@ -6,7 +6,7 @@
 
 def in_one(arrays, axis):
     vector, at, outs = (jnp.concatenate([a.reshape(-1) for a in arrays]), 0, [])
-    total = lax.psum(vector, axis)
+    total = jnp.sum(lax.all_gather(vector, axis), axis=0)
     for a in arrays:
         outs.append(total[at : at + a.size].reshape(a.shape))
         at += a.size

time: 492 us -> 1240 us (2.52)
  other arithmetic: 135 us -> 759 us
  waiting for transfers between devices: 174 us -> 298 us
    reduce_sum x0 -> x1, other arithmetic: none -> 625 us  [in_one(): total = jnp.sum(lax.all_gather(vector, axis), axis=0)]
    all_gather x0 -> x1, waiting for transfers between devices: none -> 241 us  [in_one(): total = jnp.sum(lax.all_gather(vector, axis), axis=0)]
    psum x1 -> x0, waiting for transfers between devices: 117 us -> none  [in_one(): total = lax.psum(vector, axis)]
  transfers between devices with their start and end apart: 6 -> 6, of which waited for: 5 -> 5; matrix products, arithmetic and copies ran while one was open for 38% -> 16% of each run, Pallas kernels for 0% -> 0%
where the time goes in v1:
time: 1240 us
  other arithmetic  759 us (61%)
  waiting for transfers between devices  298 us (24%)
  local copies, waits for them, and re-layouts  73.8 us (6%)
  matrix products  54.8 us (4%)
  starting transfers between devices  34 us (3%)
  between operations  15.6 us (1%)
    reduce_sum x1, other arithmetic, in_one(): total = jnp.sum(lax.all_gather(vector, axis), axis=0)  625 us
    all_gather x1, waiting for transfers between devices, in_one(): total = jnp.sum(lax.all_gather(vector, axis), axis=0)  241 us
    unnamed x4, other arithmetic  97.6 us
    slice x2, local copies, waits for them, and re-layouts, per_device(): jnp.zeros((node_rows + 1, table_rows), jnp.float32).at[dst_index, edge_src]  43.9 us
  transfers between devices with their start and end apart: 6, of which 5 were waited for; matrix products, arithmetic and copies ran while one was open for 16% of the time, Pallas kernels for 0%

profile of v1, /device:TPU:1, one launch (start us, length us, event | category | flops | bytes accessed | tf_op | source)
XLA Modules:
  0.0 1235.3 jit_solution(4298188149215909328)
XLA Ops:
  7.2 1.5 copy.31
  8.7 11.5 all-to-all-start.1
  20.8 0.8 compare_select_fusion.5
  21.8 0.9 compare_select_fusion.1
  22.6 0.9 compare_select_fusion.2
  23.5 1.0 and_reduce_fusion
  24.5 0.9 multiply_reduce_fusion
  25.4 3.0 fusion.59
  28.4 5.0 gather_fusion
  33.4 95.7 %scatter_custom_fusion.2 = f32[6294528]{0:T(1024)} fusion(s32[16384]{0:T(1024)S(1)} %broadcast_select_fusion, f32[16384]{0:T(1024)S(1)} %broadcast.84, f32[]{:T(128)} %constant.6.clone.1), kind=kCustom, calls=%fused_computation.11 | custom fusion | flops 16384 | bytes 25178116
  129.1 16.7 %slice.87 = f32[6291456]{0:T(1024)} slice(f32[6294528]{0:T(1024)} %scatter_custom_fusion.2), slice={[0:6291456]} | slice | bytes 50331648 | tf_op jit(solution)/shard_map/slice | solution.py:53
  145.8 27.2 %reshape.208 = f32[2048,3072]{1,0:T(8,128)} reshape(f32[6291456]{0:T(1024)} %slice.87) | data formatting | bytes 50331648 | tf_op jit(solution)/shard_map/slice | solution.py:53
  173.0 9.1 reduce_sum.27
  182.2 10.4 all-to-all-start
  192.7 13.7 %all-to-all-done = bf16[128,8,256]{2,1,0:T(8,128)(2,1)S(1)} async-done(((bf16[128,8,256]{2,1,0:T(8,128)(2,1)}), bf16[128,8,256]{2,1,0:T(8,128)(2,1)S(1)}, u32[]{:S(2)}, u32[]{:S(2)}) %all-to-all-start) | async-done | bytes 524320 | tf_op jit(solution)/shard_map/all_to_all | solution.py:44
  206.3 11.9 fusion.15
  218.7 9.1 gather_fusion.1
  227.7 4.1 all-to-all-start.2
  231.9 19.5 %all-to-all-done.2 = bf16[128,16,256]{2,1,0:T(8,128)(2,1)S(1)} async-done(((bf16[128,16,256]{2,1,0:T(8,128)(2,1)}), bf16[128,16,256]{2,1,0:T(8,128)(2,1)S(1)}, u32[]{:S(2)}, u32[]{:S(2)}) %all-to-all-start.2) | async-done | bytes 1048608 | tf_op jit(solution)/shard_map/all_to_all | solution.py:70
  251.4 2.9 fusion.13
  254.3 3.1 fusion.14
  257.5 0.7 convolution_add_fusion
  259.2 0.5 fusion.21
  259.8 0.8 fusion.33
  260.5 4.9 fusion
  265.5 6.2 fusion.11
  271.6 3.9 all-to-all-start.3
  275.6 0.5 broadcast.126
  276.1 0.8 reduce.8
  277.0 2.7 fusion.31
  279.7 1.1 copy.36
  281.1 14.0 %all-to-all-done.3 = bf16[128,16,256]{2,1,0:T(8,128)(2,1)S(1)} async-done(((bf16[128,16,256]{2,1,0:T(8,128)(2,1)}), bf16[128,16,256]{2,1,0:T(8,128)(2,1)S(1)}, u32[]{:S(2)}, u32[]{:S(2)}) %all-to-all-start.3) | async-done | bytes 1048608 | tf_op jit(solution)/shard_map/all_to_all | solution.py:97
  295.1 13.0 %scatter_custom_fusion = f32[2048,256]{1,0:T(8,128)} fusion(s32[2048]{0:T(1024)S(1)} %bitcast.83, bf16[2048,256]{1,0:T(8,128)(2,1)S(1)} %bitcast.66, f32[]{:T(128)} %constant.6.clone.1), kind=kCustom, calls=%fused_computation.34 | custom fusion | flops 1048576 | bytes 3145732 | tf_op jit(solution)/shard_map/scatter-add | solution.py:107
  308.1 1.7 convert_element_type.61
  309.8 0.5 convolution_bitcast_fusion
  311.4 5.7 reshape.253
  317.3 13.3 %fusion.16 = f32[3072,256]{1,0:T(8,128)} fusion(f32[2048,3072]{1,0:T(8,128)} %reshape.208, bf16[2048,256]{1,0:T(8,128)(2,1)S(1)} %convert_element_type.61, bf16[256,256]{1,0:T(8,128)(2,1)S(1)} %copy-done.8, f32[2048]{0:T(1024)S(1)} %broadcast_maximum_fusion), kind=kOutput, calls=%fused_computation.30 | convolution fusion | flops 3490185216 | bytes 29499392 | tf_op jit(solution)/shard_map/dot_general | solution.py:17
  330.6 2.2 fusion.47
  332.8 4.1 all-to-all-start.4
  336.9 3.4 convolution_add_fusion.1
  340.3 10.5 all-to-all-done.4
  350.8 9.0 scatter_custom_fusion.1
  359.7 240.6 %all-gather.4.cloned.1.call-done = f32[128,1,262656]{2,1,0:T(1,128)} async-done(((f32[1,1,262656]{2,1,0:T(1,128)}), f32[128,1,262656]{2,1,0:T(1,128)}) %all-gather.4.cloned.1.call-update) | async-done | bytes 134479888 | tf_op jit(solution)/shard_map/all_gather | solution.py:9
  600.3 624.5 %reduce_sum.29 = f32[262656]{0:T(1024)S(1)} reduce(f32[128,1,262656]{2,1,0:T(1,128)} %all-gather.4.cloned.1.call-done, f32[]{:T(128)} %constant.6.clone.1), dimensions={0,1}, to_apply=%region_5.6 | reduce | flops 33357312 | bytes 135530496 | tf_op jit(solution)/shard_map/reduce_sum | solution.py:9
  1224.9 0.6 fusion.56
  1225.5 0.8 slice.77
  1226.3 0.9 slice.79
  1227.2 0.8 slice.75
  (73 shorter events, 3.6 us)
Async XLA Ops:
  7.2 250.3 %copy-start = (bf16[512,256]{1,0:T(8,128)(2,1)S(1)}, bf16[512,256]{1,0:T(8,128)(2,1)}, u32[]{:S(2)}) copy-start(bf16[512,256]{1,0:T(8,128)(2,1)} %param.25) | copy-start | bytes 786436
  8.7 173.5 %all-to-all-start.1 = ((s32[128,1,16]{2,1,0:T(1,128)}), s32[128,1,16]{2,1,0:T(1,128)S(1)}, u32[]{:S(2)}, u32[]{:S(2)}) async-start(s32[128,1,16]{2,1,0:T(1,128)} %bitcast.7), calls=%async_computation.1 | async-start | bytes 131072 | tf_op jit(solution)/shard_map/all_to_all | solution.py:65
  20.8 7.6 copy-start.2
  182.2 24.2 %all-to-all-start = ((bf16[128,8,256]{2,1,0:T(8,128)(2,1)}), bf16[128,8,256]{2,1,0:T(8,128)(2,1)S(1)}, u32[]{:S(2)}, u32[]{:S(2)}) async-start(bf16[128,8,256]{2,1,0:T(8,128)(2,1)} %bitcast.5), calls=%async_computation | async-start | bytes 1048576 | tf_op jit(solution)/shard_map/all_to_all | solution.py:44
  206.3 11.9 copy-start.5
  206.3 11.9 copy-start.7
  227.7 4.1 copy-start.13
  227.7 23.7 %all-to-all-start.2 = ((bf16[128,16,256]{2,1,0:T(8,128)(2,1)}), bf16[128,16,256]{2,1,0:T(8,128)(2,1)S(1)}, u32[]{:S(2)}, u32[]{:S(2)}) async-start(bf16[128,16,256]{2,1,0:T(8,128)(2,1)} %bitcast.65), calls=%async_computation.2 | async-start | bytes 2097152 | tf_op jit(solution)/shard_map/all_to_all | solution.py:70
  254.3 3.1 copy-start.18
  254.3 3.1 copy-start.17
  257.4 1.0 copy-start.19
  257.5 1.0 copy-start.16
  258.4 1.3 copy-start.3
  258.4 0.7 copy-start.14
  258.4 0.8 copy-start.15
  258.8 1.7 copy-start.11
  259.8 5.7 copy-start.9
  271.6 23.4 %all-to-all-start.3 = ((bf16[128,16,256]{2,1,0:T(8,128)(2,1)}), bf16[128,16,256]{2,1,0:T(8,128)(2,1)S(1)}, u32[]{:S(2)}, u32[]{:S(2)}) async-start(bf16[128,16,256]{2,1,0:T(8,128)(2,1)} %bitcast.69), calls=%async_computation.3 | async-start | bytes 2097152 | tf_op jit(solution)/shard_map/all_to_all | solution.py:97
  275.5 324.8 %all-gather.4.cloned.1.call-start = ((), (), s32[]{:S(2)}) async-start(), calls=%async_computation.5 | async-start | bytes 135530496 | tf_op jit(solution)/shard_map/all_gather | solution.py:9
  277.0 3.8 copy-start.4
  310.3 1.0 copy-start.6
  311.3 5.8 copy-start.12
  311.3 6.0 copy-start.8
  330.6 6.3 copy-start.10
  332.8 18.0 %all-to-all-start.4 = ((bf16[128,8,256]{2,1,0:T(8,128)(2,1)}), bf16[128,8,256]{2,1,0:T(8,128)(2,1)S(1)}, u32[]{:S(2)}, u32[]{:S(2)}) async-start(bf16[128,8,256]{2,1,0:T(8,128)(2,1)} %fusion.47), calls=%async_computation.4 | async-start | bytes 1048576 | tf_op jit(solution)/shard_map/all_to_all | solution.py:116
  1224.9 3.2 copy-start.1
Sparse Core Ops, SparseCore 0:
  317.2 283.0 all-gather.3
